TPU v7x, 32 devices: a 4x2x2 block of a 4x4x8 slice. The times are simulated.
32 devices in a mesh: dp: 4 (over y, z), sp: 8 (over x, core).
Axes of the slice: x: 4, y: 2, z: 2, core: 2. Of those that a mesh axis runs over, the one named last changes fastest.
The devices are a block of a 4x4x8 slice.
Arguments:
- x: bfloat16 [64, 1536, 512], P('dp', 'sp'), parts along dimension 0
- ln1_gain: bfloat16 [512], replicated
- ln1_bias: bfloat16 [512], replicated
- w_query: bfloat16 [512, 512], replicated
- b_query: bfloat16 [512], replicated
- w_key: bfloat16 [512, 512], replicated
- w_value: bfloat16 [512, 512], replicated
- b_value: bfloat16 [512], replicated
- w_out: bfloat16 [512, 512], replicated
- b_out: bfloat16 [512], replicated
- ln2_gain: bfloat16 [512], replicated
- ln2_bias: bfloat16 [512], replicated
- w_up: bfloat16 [512, 2048], replicated
- b_up: bfloat16 [2048], replicated
- w_down: bfloat16 [2048, 512], replicated
- b_down: bfloat16 [512], replicated
- lnp_gain: bfloat16 [512], replicated
- lnp_bias: bfloat16 [512], replicated
- cross_wk: bfloat16 [6, 512, 512], P(None, None, 'sp')
- cross_wv: bfloat16 [6, 512, 512], P(None, None, 'sp')
- cross_bv: bfloat16 [6, 512], P(None, 'sp')
Outputs:
- output 1: bfloat16 [6, 64, 1536, 8, 64], P(None, 'dp', None, 'sp'), parts along dimension 1
- output 2: bfloat16 [6, 64, 1536, 8, 64], P(None, 'dp', None, 'sp'), parts along dimension 1
There are 4 independent parts. A program takes and returns all parts, laid end to end along the dimension named above; an argument that names none is the same for every part.
All inputs are finite; a program needn't handle non-finite values.
Results may differ from a plain program's by a relative error of at most 0.00610293.
Values are sent between devices in bfloat16 or wider.
A program may use at most 768 MiB of HBM per device.

v0:
```python
import jax
import jax.numpy as jnp
from jax import lax
from jax.sharding import PartitionSpec as P

HEAD_DIM = 64
LN_EPS = 1e-5


def layer_norm(hidden_in, ln_gain, ln_bias):
    mean_val = jnp.mean(hidden_in, axis=-1, keepdims=True)
    centered = hidden_in - mean_val
    variance = jnp.mean(centered * centered, axis=-1, keepdims=True)
    return centered * lax.rsqrt(variance + LN_EPS) * ln_gain.astype(jnp.float32) + ln_bias.astype(jnp.float32)


def solution(mesh):
    def device_fn(x_rows, ln1_gain, ln1_bias, w_query, b_query, w_key, w_value, b_value, w_out, b_out, ln2_gain, ln2_bias, w_up, b_up, w_down, b_down, lnp_gain, lnp_bias, cross_wk, cross_wv, cross_bv):
        batch_rows, frames_dev, d_model = x_rows.shape
        num_heads = d_model // HEAD_DIM
        num_layers = cross_wk.shape[0]
        heads_dev = cross_wk.shape[2] // HEAD_DIM
        qk_scale = HEAD_DIM ** -0.25
        residual = x_rows.astype(jnp.float32)
        normed = layer_norm(residual, ln1_gain, ln1_bias).astype(jnp.bfloat16)
        queries = ((jnp.einsum('bfd,de->bfe', normed, w_query, preferred_element_type=jnp.float32) + b_query.astype(jnp.float32)) * qk_scale).astype(jnp.bfloat16)
        key_rows = (jnp.einsum('bfd,de->bfe', normed, w_key, preferred_element_type=jnp.float32) * qk_scale).astype(jnp.bfloat16)
        value_rows = (jnp.einsum('bfd,de->bfe', normed, w_value, preferred_element_type=jnp.float32) + b_value.astype(jnp.float32)).astype(jnp.bfloat16)
        key_all = lax.all_gather(key_rows, 'sp', axis=1, tiled=True)
        value_all = lax.all_gather(value_rows, 'sp', axis=1, tiled=True)
        frames_all = key_all.shape[1]
        q_heads = queries.reshape(batch_rows, frames_dev, num_heads, HEAD_DIM)
        k_heads = key_all.reshape(batch_rows, frames_all, num_heads, HEAD_DIM)
        v_heads = value_all.reshape(batch_rows, frames_all, num_heads, HEAD_DIM)
        scores = jnp.einsum('bqhc,bkhc->bhqk', q_heads, k_heads, preferred_element_type=jnp.float32)
        attn_probs = jax.nn.softmax(scores, axis=-1).astype(jnp.bfloat16)
        attended = jnp.einsum('bhqk,bkhc->bqhc', attn_probs, v_heads, preferred_element_type=jnp.float32).astype(jnp.bfloat16)
        attended = attended.reshape(batch_rows, frames_dev, d_model)
        residual = residual + jnp.einsum('bfd,de->bfe', attended, w_out, preferred_element_type=jnp.float32) + b_out.astype(jnp.float32)
        normed = layer_norm(residual, ln2_gain, ln2_bias).astype(jnp.bfloat16)
        hidden = jax.nn.gelu(jnp.einsum('bfd,de->bfe', normed, w_up, preferred_element_type=jnp.float32) + b_up.astype(jnp.float32), approximate=False).astype(jnp.bfloat16)
        residual = residual + jnp.einsum('bfe,ed->bfd', hidden, w_down, preferred_element_type=jnp.float32) + b_down.astype(jnp.float32)
        y_local = layer_norm(residual, lnp_gain, lnp_bias).astype(jnp.bfloat16)
        y_all = lax.all_gather(y_local, 'sp', axis=1, tiled=True)
        wk_heads = cross_wk.reshape(num_layers, d_model, heads_dev, HEAD_DIM)
        wv_heads = cross_wv.reshape(num_layers, d_model, heads_dev, HEAD_DIM)
        bv_heads = cross_bv.reshape(num_layers, 1, 1, heads_dev, HEAD_DIM).astype(jnp.float32)
        k_cache = jnp.einsum('bfd,ldhc->lbfhc', y_all, wk_heads, preferred_element_type=jnp.float32).astype(jnp.bfloat16)
        v_cache = (jnp.einsum('bfd,ldhc->lbfhc', y_all, wv_heads, preferred_element_type=jnp.float32) + bv_heads).astype(jnp.bfloat16)
        return k_cache, v_cache

    in_specs = (P('dp', 'sp', None),) + (P(),) * 17 + (P(None, None, 'sp'), P(None, None, 'sp'), P(None, 'sp'))
    out_specs = (P(None, 'dp', None, 'sp', None), P(None, 'dp', None, 'sp', None))
    return jax.shard_map(device_fn, mesh=mesh, in_specs=in_specs, out_specs=out_specs, check_vma=False)
```

profile of v0, /device:TPU:81, one launch (start us, length us, event | category | flops | bytes accessed | tf_op | source)
XLA Modules:
  0.0 682.3 jit_solution(8135900703931134118)
XLA Ops:
  7.2 0.0 copy-start
  7.2 0.0 copy-start.12
  7.2 0.0 copy-start.20
  7.2 0.1 all-gather.6.cloned.1.call-start
  7.3 2.7 convert_reduce_fusion
  10.0 2.9 fusion.29
  12.9 0.7 convert_element_type.89
  13.5 0.7 convert_element_type.90
  14.2 5.0 multiply_convert_fusion
  19.3 0.0 copy-start.15
  19.3 0.0 copy-start.16
  19.3 0.0 copy-start.17
  19.3 0.0 copy-start.18
  19.3 0.1 all-gather.6.cloned.1.call-update
  19.4 0.1 all-gather.4.cloned.1.call-start
  19.5 0.7 convert_element_type.92
  20.1 4.9 add_convert_fusion.2
  25.1 0.1 all-gather.4.cloned.1.call-update
  25.1 0.4 all-gather.8.cloned.1.call-start
  25.6 0.0 copy-done.12
  25.6 0.0 copy-done.20
  25.6 4.9 multiply_convert_fusion.1
  30.5 5.9 copy.30
  36.5 0.0 copy-done.13
  36.5 0.6 convert_element_type.100
  37.1 0.0 copy-done.6
  37.1 0.6 convert_element_type.104
  37.7 0.0 copy-done.14
  37.7 0.6 convert_element_type.101
  38.2 0.0 copy-done.15
  38.2 0.6 convert_element_type.102
  38.8 0.0 copy-done.16
  38.8 0.6 convert_element_type.106
  39.4 0.0 copy-done.17
  39.4 0.6 convert_element_type.107
  39.9 0.0 copy-done.18
  39.9 0.6 convert_element_type.108
  40.5 101.3 %all-gather.6.cloned.1.call-done = bf16[16,1536,512]{2,1,0:T(8,128)(2,1)} async-done(((bf16[16,192,512]{2,1,0:T(8,128)(2,1)}), bf16[16,1536,512]{2,1,0:T(8,128)(2,1)}) %all-gather.6.cloned.1.call-update) | async-done | bytes 25165840 | tf_op jit(solution)/shard_map/all_gather | solution.py:29
  141.8 32.6 %copy.31 = bf16[16,1536,512]{1,2,0:T(8,128)(2,1)} copy(bf16[16,1536,512]{2,1,0:T(8,128)(2,1)} %all-gather.6.cloned.1.call-done) | data formatting | bytes 50331648 | tf_op jit(solution)/shard_map/all_gather | solution.py:29
  174.4 67.6 %fusion.86 = (f32[16,8,192]{2,1,0:T(8,128)S(1)}, f32[16,8,192,1536]{3,2,1,0:T(8,128)}) fusion(bf16[16,192,8,64]{1,3,2,0:T(8,128)(2,1)} %bitcast.71, bf16[16,1536,8,64]{1,3,2,0:T(8,128)(2,1)} %bitcast.69), kind=kOutput, calls=%fused_computation.109 | convolution fusion | flops 4907337216 | bytes 179404800 | tf_op jit(solution)/shard_map/sub | solution.py:36
  242.0 20.6 %all-gather.4.cloned.1.call-done = bf16[16,1536,512]{2,1,0:T(8,128)(2,1)} async-done(((bf16[16,192,512]{2,1,0:T(8,128)(2,1)}), bf16[16,1536,512]{2,1,0:T(8,128)(2,1)}) %all-gather.4.cloned.1.call-update) | async-done | bytes 25165840 | tf_op jit(solution)/shard_map/all_gather | solution.py:30
  262.6 32.6 %copy.29 = bf16[16,1536,512]{1,2,0:T(8,128)(2,1)} copy(bf16[16,1536,512]{2,1,0:T(8,128)(2,1)} %all-gather.4.cloned.1.call-done) | data formatting | bytes 50331648 | tf_op jit(solution)/shard_map/all_gather | solution.py:30
  295.2 0.0 copy-start.9
  295.3 0.0 copy-start.10
  295.3 57.3 %fusion.41 = bf16[16,8,64,192]{3,2,1,0:T(8,128)(2,1)} fusion(bf16[16,1536,8,64]{1,3,2,0:T(8,128)(2,1)} %bitcast.70, f32[16,8,192,1536]{3,2,1,0:T(8,128)} %get-tuple-element.9, f32[16,8,192]{2,1,0:T(8,128)S(1)} %get-tuple-element.8), kind=kOutput, calls=%fused_computation.63 | convolution fusion | flops 4908908544 | bytes 179404800 | tf_op jit(solution)/shard_map/bhqk,bkhc->bqhc/dot_general | solution.py:37
  352.6 0.0 copy-done.2
  352.6 0.0 copy-done.11
  352.6 0.0 copy-done.21
  352.6 4.4 fusion.87
  357.0 1.2 multiply_reduce_fusion.1
  358.3 0.0 copy-start.19
  358.4 16.3 %fusion.24 = (u16[192,2048]{1,0:T(8,128)(2,1)S(1)}, u16[192,2048]{1,0:T(8,128)(2,1)S(1)}, f32[16,192,2048]{2,1,0:T(8,128)}) fusion(f32[2048]{0:T(1024)S(1)} %copy-done.5, bf16[512,2048]{1,0:T(8,128)(2,1)S(1)} %copy-done, f32[16,192,512]{2,1,0:T(8,128)S(1)} %get-tuple-element.11, f32[512]{0:T(512)S(1)} %copy-done.10, f32[512]{0:T(512)S(1)} %copy-done.9, ...), kind=kOutput, calls=%fused_computation.36 | convolution fusion | flops 6537609216 | bytes 35164160 | tf_op jit(solution)/shard_map/bfd,de->bfe/dot_general | solution.py:41
  374.7 0.0 copy-start.7
  374.7 0.0 copy-start.22
  374.8 73.0 %fusion.88 = (f32[16,192]{1,0:T(8,128)S(1)}, f32[16,192,512]{2,1,0:T(8,128)S(1)}) fusion(f32[512]{0:T(512)S(1)} %copy-done.8, f32[16,192,512]{2,1,0:T(8,128)S(1)} %get-tuple-element.11, bf16[2048,512]{1,0:T(8,128)(2,1)S(1)} %copy-done.19, f32[16,192,2048]{2,1,0:T(8,128)} %get-tuple-element.12, f32[2048]{0:T(1024)S(1)} %copy-done.5, ...), kind=kOutput, calls=%fused_computation.111 | convolution fusion | flops 6893859840 | bytes 41441280 | tf_op jit(solution)/shard_map/bfe,ed->bfd/dot_general | solution.py:42
  447.8 1.2 multiply_reduce_fusion
  449.1 2.3 add_convert_fusion
  451.4 0.1 all-gather.8.cloned.1.call-update
  451.4 118.7 %all-gather.8.cloned.1.call-done = bf16[16,1536,512]{2,1,0:T(8,128)(2,1)} async-done(((bf16[16,192,512]{2,1,0:T(8,128)(2,1)}), bf16[16,1536,512]{2,1,0:T(8,128)(2,1)}) %all-gather.8.cloned.1.call-update) | async-done | bytes 25165840 | tf_op jit(solution)/shard_map/all_gather | solution.py:44
  570.2 35.9 %fusion.16 = bf16[6,16,1536,1,64]{2,4,0,1,3:T(8,128)(2,1)} fusion(f32[6,64]{1,0:T(8,128)S(1)} %convert_element_type.114, bf16[16,1536,512]{2,1,0:T(8,128)(2,1)} %all-gather.8.cloned.1.call-done, bf16[6,512,64]{1,2,0:T(8,128)(2,1)S(1)} %copy-done.22), kind=kOutput, calls=%fused_computation.32 | convolution fusion | flops 9682550784 | bytes 44434944 | tf_op jit(solution)/shard_map/bfd,ldhc->lbfhc/dot_general | solution.py:49
  606.1 17.0 %copy.34 = bf16[6,16,1536,1,64]{2,4,3,1,0:T(8,128)(2,1)} copy(bf16[6,16,1536,1,64]{2,4,0,1,3:T(8,128)(2,1)} %fusion.16) | data formatting | bytes 37748736
  623.1 0.0 copy-done.23
  623.1 35.4 %convert_bitcast_fusion = bf16[6,16,1536,1,64]{2,4,0,1,3:T(8,128)(2,1)} fusion(bf16[16,1536,512]{2,1,0:T(8,128)(2,1)} %all-gather.8.cloned.1.call-done, bf16[6,512,64]{1,2,0:T(8,128)(2,1)S(1)} %copy-done.23), kind=kOutput, calls=%fused_computation.33 | convolution fusion | flops 9673113600 | bytes 44433408 | tf_op jit(solution)/shard_map/bfd,ldhc->lbfhc/dot_general | solution.py:48
  658.5 17.0 %copy.33 = bf16[6,16,1536,1,64]{2,4,3,1,0:T(8,128)(2,1)} copy(bf16[6,16,1536,1,64]{2,4,0,1,3:T(8,128)(2,1)} %convert_bitcast_fusion) | data formatting | bytes 37748736
  (31 shorter events, 0.1 us)
Async XLA Ops:
  7.2 351.1 %copy-start = (bf16[512,2048]{1,0:T(8,128)(2,1)S(1)}, bf16[512,2048]{1,0:T(8,128)(2,1)}, u32[]{:S(2)}) copy-start(bf16[512,2048]{1,0:T(8,128)(2,1)} %param.33) | copy-start | bytes 6291460
  7.2 18.4 %copy-start.12 = (bf16[512]{0:T(512)(128)(2,1)S(1)}, bf16[512]{0:T(512)(128)(2,1)}, u32[]{:S(2)}) copy-start(bf16[512]{0:T(512)(128)(2,1)} %param.25) | copy-start | bytes 3076
  7.2 18.4 %copy-start.20 = (bf16[512,512]{1,0:T(8,128)(2,1)S(1)}, bf16[512,512]{1,0:T(8,128)(2,1)}, u32[]{:S(2)}) copy-start(bf16[512,512]{1,0:T(8,128)(2,1)} %param.24) | copy-start | bytes 1572868
  7.2 134.6 %all-gather.6.cloned.1.call-start = ((), (), s32[]{:S(2)}) async-start(), calls=%async_computation.1 | async-start | bytes 28311552 | tf_op jit(solution)/shard_map/all_gather | solution.py:29
  19.3 17.2 %copy-start.13 = (bf16[512]{0:T(512)(128)(2,1)S(1)}, bf16[512]{0:T(512)(128)(2,1)}, u32[]{:S(2)}) copy-start(bf16[512]{0:T(512)(128)(2,1)} %param.30) | copy-start | bytes 3076
  19.3 17.8 %copy-start.6 = (bf16[2048]{0:T(1024)(128)(2,1)S(1)}, bf16[2048]{0:T(1024)(128)(2,1)}, u32[]{:S(2)}) copy-start(bf16[2048]{0:T(1024)(128)(2,1)} %param.34) | copy-start | bytes 12292
  19.3 18.4 %copy-start.14 = (bf16[512]{0:T(512)(128)(2,1)S(1)}, bf16[512]{0:T(512)(128)(2,1)}, u32[]{:S(2)}) copy-start(bf16[512]{0:T(512)(128)(2,1)} %param.31) | copy-start | bytes 3076
  19.3 19.0 %copy-start.15 = (bf16[512]{0:T(512)(128)(2,1)S(1)}, bf16[512]{0:T(512)(128)(2,1)}, u32[]{:S(2)}) copy-start(bf16[512]{0:T(512)(128)(2,1)} %param.32) | copy-start | bytes 3076
  19.3 19.5 %copy-start.16 = (bf16[512]{0:T(512)(128)(2,1)S(1)}, bf16[512]{0:T(512)(128)(2,1)}, u32[]{:S(2)}) copy-start(bf16[512]{0:T(512)(128)(2,1)} %param.36) | copy-start | bytes 3076
  19.3 20.1 %copy-start.17 = (bf16[512]{0:T(512)(128)(2,1)S(1)}, bf16[512]{0:T(512)(128)(2,1)}, u32[]{:S(2)}) copy-start(bf16[512]{0:T(512)(128)(2,1)} %param.37) | copy-start | bytes 3076
  19.3 20.6 %copy-start.18 = (bf16[512]{0:T(512)(128)(2,1)S(1)}, bf16[512]{0:T(512)(128)(2,1)}, u32[]{:S(2)}) copy-start(bf16[512]{0:T(512)(128)(2,1)} %param.38) | copy-start | bytes 3076
  19.4 243.2 %all-gather.4.cloned.1.call-start = ((), (), s32[]{:S(2)}) async-start(), calls=%async_computation | async-start | bytes 28311552 | tf_op jit(solution)/shard_map/all_gather | solution.py:30
  25.1 545.0 %all-gather.8.cloned.1.call-start = ((), (), s32[]{:S(2)}) async-start(), calls=%async_computation.2 | async-start | bytes 28311552 | tf_op jit(solution)/shard_map/all_gather | solution.py:44
  295.2 57.3 %copy-start.2 = (bf16[16,192,512]{2,1,0:T(8,128)(2,1)S(1)}, bf16[16,192,512]{2,1,0:T(8,128)(2,1)}, u32[]{:S(2)}) copy-start(bf16[16,192,512]{2,1,0:T(8,128)(2,1)} %param.21) | copy-start | bytes 9437188
  295.2 57.3 %copy-start.11 = (f32[512]{0:T(512)S(1)}, f32[512]{0:T(512)}, u32[]{:S(2)}) copy-start(f32[512]{0:T(512)} %convert_element_type.100) | copy-start | bytes 6148
  295.2 57.3 %copy-start.21 = (bf16[512,512]{1,0:T(8,128)(2,1)S(1)}, bf16[512,512]{1,0:T(8,128)(2,1)}, u32[]{:S(2)}) copy-start(bf16[512,512]{1,0:T(8,128)(2,1)} %param.29) | copy-start | bytes 1572868
  295.2 63.1 %copy-start.5 = (f32[2048]{0:T(1024)S(1)}, f32[2048]{0:T(1024)}, u32[]{:S(2)}) copy-start(f32[2048]{0:T(1024)} %convert_element_type.104) | copy-start | bytes 24580
  295.2 63.1 %copy-start.9 = (f32[512]{0:T(512)S(1)}, f32[512]{0:T(512)}, u32[]{:S(2)}) copy-start(f32[512]{0:T(512)} %convert_element_type.101) | copy-start | bytes 6148
  295.3 63.1 %copy-start.10 = (f32[512]{0:T(512)S(1)}, f32[512]{0:T(512)}, u32[]{:S(2)}) copy-start(f32[512]{0:T(512)} %convert_element_type.102) | copy-start | bytes 6148
  358.3 16.4 %copy-start.8 = (f32[512]{0:T(512)S(1)}, f32[512]{0:T(512)}, u32[]{:S(2)}) copy-start(f32[512]{0:T(512)} %convert_element_type.106) | copy-start | bytes 6148
  358.3 16.4 %copy-start.19 = (bf16[2048,512]{1,0:T(8,128)(2,1)S(1)}, bf16[2048,512]{1,0:T(8,128)(2,1)}, u32[]{:S(2)}) copy-start(bf16[2048,512]{1,0:T(8,128)(2,1)} %param.35) | copy-start | bytes 6291460
  374.7 74.4 %copy-start.3 = (f32[512]{0:T(512)S(1)}, f32[512]{0:T(512)}, u32[]{:S(2)}) copy-start(f32[512]{0:T(512)} %convert_element_type.107) | copy-start | bytes 6148
  374.7 74.4 %copy-start.4 = (f32[512]{0:T(512)S(1)}, f32[512]{0:T(512)}, u32[]{:S(2)}) copy-start(f32[512]{0:T(512)} %convert_element_type.108) | copy-start | bytes 6148
  374.7 76.7 %copy-start.7 = (bf16[6,64]{1,0:T(8,128)(2,1)S(1)}, bf16[6,64]{1,0:T(8,128)(2,1)}, u32[]{:S(2)}) copy-start(bf16[6,64]{1,0:T(8,128)(2,1)} %param.41) | copy-start | bytes 2308
  374.7 195.4 %copy-start.22 = (bf16[6,512,64]{1,2,0:T(8,128)(2,1)S(1)}, bf16[6,512,64]{1,2,0:T(8,128)(2,1)}, u32[]{:S(2)}) copy-start(bf16[6,512,64]{1,2,0:T(8,128)(2,1)} %param.40) | copy-start | bytes 1179652
  606.1 17.0 %copy-start.23 = (bf16[6,512,64]{1,2,0:T(8,128)(2,1)S(1)}, bf16[6,512,64]{1,2,0:T(8,128)(2,1)}, u32[]{:S(2)}) copy-start(bf16[6,512,64]{1,2,0:T(8,128)(2,1)} %param.39) | copy-start | bytes 1179652
  623.1 52.4 %copy-start.1 = (bf16[512,2048]{1,0:T(8,128)(2,1)S(1)}, bf16[512,2048]{1,0:T(8,128)(2,1)}, u32[]{:S(2)}) copy-start(bf16[512,2048]{1,0:T(8,128)(2,1)} %param.33) | copy-start | bytes 6291460
Sparse Core Ops, SparseCore 0:
  19.5 122.2 all-gather.5
  144.0 118.5 all-gather.3
  451.5 118.5 all-gather.7
where the time goes:
time: 683 us; the launch traced here: 682 us
  matrix products  305 us (45%)
  waiting for transfers between devices  241 us (35%)
  local copies, waits for them, and re-layouts  105 us (15%)
  other arithmetic  16.4 us (2%)
  between operations  14.3 us (2%)
    all_gather x1, waiting for transfers between devices, device_fn(): y_all = lax.all_gather(y_local, 'sp', axis=1, tiled=True)  119 us
    all_gather x1, waiting for transfers between devices, device_fn(): key_all = lax.all_gather(key_rows, 'sp', axis=1, tiled=True)  101 us
    dot_general x1, matrix products, device_fn(): jnp.einsum('bfe,ed->bfd', hidden, w_down, preferred_element_type=jnp.floa...  73 us
    sub x1, matrix products, device_fn(): attn_probs = jax.nn.softmax(scores, axis=-1).astype(jnp.bfloat16)  67.6 us
    dot_general x1, matrix products, device_fn(): jnp.einsum('bhqk,bkhc->bqhc', attn_probs, v_heads, preferred_element_type...  57.3 us
    dot_general x1, matrix products, device_fn(): jnp.einsum('bfd,ldhc->lbfhc', y_all, wv_heads, preferred_element_type=jnp...  35.9 us
    dot_general x1, matrix products, device_fn(): jnp.einsum('bfd,ldhc->lbfhc', y_all, wk_heads, preferred_element_type=jnp...  35.4 us
    unnamed x50, local copies, waits for them, and re-layouts  34.1 us
  transfers between devices with their start and end apart: 3, of which 3 were waited for; matrix products, arithmetic and copies ran while one was open for 18% of the time, Pallas kernels for 0%

commit v1 on v0

v1 whole, which is shorter than its diff:
```python
import functools
import jax
import jax.numpy as jnp
from jax import lax
from jax.experimental import pallas as pl
from jax.experimental.pallas import tpu as pltpu
from jax.sharding import PartitionSpec as P

HEAD_DIM = 64
LN_EPS = 1e-5
SQRT_HALF = 0.5 ** 0.5
PAIR = 2 * HEAD_DIM
VMEM_BYTES = 63 * 1024 * 1024
CORES = 2
MESH_ID = pl.DeviceIdType.MESH
NT = (((1,), (1,)), ((), ()))


def norm_rows(rows, gain, bias):
    mean_val = jnp.mean(rows, axis=-1, keepdims=True)
    centered = rows - mean_val
    variance = jnp.mean(centered * centered, axis=-1, keepdims=True)
    return centered * lax.rsqrt(variance + LN_EPS) * gain + bias


def f32(ref):
    return ref[...].astype(jnp.float32)


def vec(ref):
    return f32(ref).reshape(1, ref.shape[0])


def encoder_kernel(x_hbm, wq_hbm, wk_hbm, wv_hbm, wo_hbm, wu_hbm, wd_hbm,
                   gain1_ref, bias1_ref, bq_ref, bv_ref, bo_ref, gain2_ref, bias2_ref, bu_ref, bd_ref, gainp_ref, biasp_ref,
                   y_all, a_all, x_buf, y_buf, wq_ref, wk_ref, wkt_ref, wv_ref, wo_ref, wu_ref, wd_ref, kt_ref, v_ref, att_ref,
                   load_sem, keep_sem, a_send, a_recv, y_send, y_recv):
    clips, frames, d_model = x_hbm.shape
    chips = y_all.shape[2]
    half = frames // 2
    me = lax.axis_index('sp')
    core, chip = lax.rem(me, CORES), lax.div(me, CORES)
    other = 1 - core
    rchip, lchip, far = lax.rem(chip + 1, chips), lax.rem(chip + chips - 1, chips), lax.rem(chip + 2, chips)
    right, left, partner = {'sp': rchip * CORES + core}, {'sp': lchip * CORES + core}, {'sp': chip * CORES + other}

    loads = [pltpu.make_async_copy(x_hbm.at[pl.ds(0, 2)], x_buf.at[pl.ds(0, 2)], load_sem.at[0]),
             pltpu.make_async_copy(x_hbm.at[pl.ds(2, clips - 2)], x_buf.at[pl.ds(2, clips - 2)], load_sem.at[1])]
    pairs = ((wq_hbm, wq_ref), (wk_hbm, wk_ref), (wv_hbm, wv_ref), (wo_hbm, wo_ref), (wu_hbm, wu_ref), (wd_hbm, wd_ref))
    loads += [pltpu.make_async_copy(src, dst, load_sem.at[2 + i]) for i, (src, dst) in enumerate(pairs)]
    for load in loads:
        load.start()

    barrier = pltpu.get_barrier_semaphore()
    for peer in (left, right, partner):
        pl.semaphore_signal(barrier, inc=1, device_id=peer, device_id_type=MESH_ID)
    pl.semaphore_wait(barrier, 3)

    def remote(src, dst, send, recv, peer):
        return pltpu.make_async_remote_copy(src_ref=src, dst_ref=dst, send_sem=send, recv_sem=recv, device_id=peer, device_id_type=MESH_ID)

    def ring(buf, send, recv, own):
        def shard(clip, where):
            return buf.at[clip, core, where]

        def lower(clip, where):
            return buf.at[clip, core, where, pl.ds(0, half)]

        def upper(clip, where):
            return buf.at[clip, core, where, pl.ds(half, half)]

        def out_right(clip):
            return remote(own(clip), shard(clip, chip), send.at[0, clip], recv.at[0, clip], right)

        def out_left(clip):
            return remote(own(clip), shard(clip, chip), send.at[1, clip], recv.at[1, clip], left)

        def fwd_right(clip):
            return remote(lower(clip, lchip), lower(clip, lchip), send.at[2, clip], recv.at[2, clip], right)

        def fwd_left(clip):
            return remote(upper(clip, rchip), upper(clip, rchip), send.at[3, clip], recv.at[3, clip], left)

        def across(clip):
            return remote(buf.at[clip, core], buf.at[clip, core], send.at[4, clip], recv.at[4, clip], partner)

        def first(clip):
            out_right(clip).start()
            out_left(clip).start()

        def relay(clip):
            remote(shard(clip, lchip), shard(clip, lchip), send.at[0, clip], recv.at[0, clip], right).wait_recv()
            fwd_right(clip).start()
            remote(shard(clip, rchip), shard(clip, rchip), send.at[1, clip], recv.at[1, clip], left).wait_recv()
            fwd_left(clip).start()

        def push(clip):
            remote(lower(clip, far), lower(clip, far), send.at[2, clip], recv.at[2, clip], right).wait_recv()
            remote(upper(clip, far), upper(clip, far), send.at[3, clip], recv.at[3, clip], left).wait_recv()
            across(clip).start()

        def finish(clip):
            remote(buf.at[clip, other], buf.at[clip, other], send.at[4, clip], recv.at[4, clip], partner).wait_recv()

        def sent(clip):
            for copy in (out_right(clip), out_left(clip), fwd_right(clip), fwd_left(clip), across(clip)):
                copy.wait_send()

        return first, relay, push, finish, sent

    a_first, a_relay, a_push, a_finish, a_sent = ring(a_all, a_send, a_recv, lambda clip: a_all.at[clip, core, chip])
    y_first, y_relay, y_push, y_finish, y_sent = ring(y_all, y_send, y_recv, lambda clip: y_buf.at[clip])

    def keep(clip):
        return pltpu.make_async_copy(y_buf.at[clip], y_all.at[clip, core, chip], keep_sem.at[clip])

    gain1, bias1 = vec(gain1_ref), vec(bias1_ref)

    def norm(clip):
        a_all[clip, core, chip] = norm_rows(x_buf[clip].astype(jnp.float32), gain1, bias1).astype(jnp.bfloat16)

    def norm_range(lo, hi):
        @pl.loop(lo, hi)
        def _(clip):
            norm(clip)

    loads[0].wait()
    norm(0)
    norm(1)
    a_first(0)
    a_first(1)
    loads[1].wait()
    third = (clips - 2) // 3
    norm_range(2, 2 + third)
    a_relay(0)
    a_first(2)
    norm_range(2 + third, 2 + 2 * third)
    a_relay(1)
    a_first(3)
    norm_range(2 + 2 * third, clips)
    for load in loads[2:]:
        load.wait()
    wkt_ref[...] = wk_ref[...].T
    a_push(0)

    qk_scale = HEAD_DIM ** -0.25
    low = lax.broadcasted_iota(jnp.int32, (frames, PAIR), 1) < HEAD_DIM

    def attention(clip):
        own = a_all[clip, core, chip]
        rows = a_all[clip].reshape(CORES * chips * frames, d_model)
        queries = ((jnp.dot(own, wq_ref[...], preferred_element_type=jnp.float32) + vec(bq_ref)) * qk_scale).astype(jnp.bfloat16)
        kt_ref[...] = (lax.dot_general(wkt_ref[...], rows, NT, preferred_element_type=jnp.float32) * qk_scale).astype(jnp.bfloat16)
        v_ref[...] = (jnp.dot(rows, wv_ref[...], preferred_element_type=jnp.float32) + vec(bv_ref)).astype(jnp.bfloat16)
        for pair in range(d_model // PAIR):
            cols = slice(pair * PAIR, (pair + 1) * PAIR)
            q_pair = queries[:, cols]
            kt_pair = kt_ref[cols, :]
            v_pair = v_ref[:, cols]
            parts = []
            for side in range(2):
                q_head = jnp.where(low if side == 0 else jnp.logical_not(low), q_pair, jnp.zeros_like(q_pair))
                scores = jnp.dot(q_head, kt_pair, preferred_element_type=jnp.float32)
                top = jnp.max(scores, axis=-1, keepdims=True)
                weights = jnp.exp(scores - top)
                total = jnp.sum(weights, axis=-1, keepdims=True)
                mixed = jnp.dot(weights.astype(jnp.bfloat16), v_pair, preferred_element_type=jnp.float32)
                parts.append(mixed / total)
            att_ref[:, cols] = jnp.where(low, parts[0], parts[1]).astype(jnp.bfloat16)

    def feed_forward(clip):
        residual = x_buf[clip].astype(jnp.float32)
        residual = residual + jnp.dot(att_ref[...], wo_ref[...], preferred_element_type=jnp.float32) + vec(bo_ref)
        normed = norm_rows(residual, vec(gain2_ref), vec(bias2_ref)).astype(jnp.bfloat16)
        acc = residual
        for start in range(0, wu_ref.shape[1], d_model):
            cols = slice(start, start + d_model)
            up = jnp.dot(normed, wu_ref[:, cols], preferred_element_type=jnp.float32) + bu_ref[cols].astype(jnp.float32).reshape(1, d_model)
            hidden = (0.5 * up * (1.0 + lax.erf(up * SQRT_HALF))).astype(jnp.bfloat16)
            acc = acc + jnp.dot(hidden, wd_ref[cols, :], preferred_element_type=jnp.float32)
        acc = acc + vec(bd_ref)
        y_buf[clip] = norm_rows(acc, vec(gainp_ref), vec(biasp_ref)).astype(jnp.bfloat16)

    @pl.loop(0, clips)
    def _(clip):
        @pl.when(clip + 2 < clips)
        def _():
            a_relay(clip + 2)

        @pl.when(clip + 4 < clips)
        def _():
            a_first(clip + 4)

        @pl.when(clip + 1 < clips)
        def _():
            a_push(clip + 1)

        a_finish(clip)
        attention(clip)

        @pl.when(clip >= 1)
        def _():
            y_relay(clip - 1)

        feed_forward(clip)
        keep(clip).start()
        y_first(clip)

        @pl.when(clip >= 2)
        def _():
            keep(clip - 2).wait()
            y_push(clip - 2)

    y_relay(clips - 1)
    keep(clips - 2).wait()
    y_push(clips - 2)
    keep(clips - 1).wait()
    y_push(clips - 1)

    @pl.loop(0, clips)
    def _(clip):
        y_finish(clip)
        a_sent(clip)
        y_sent(clip)


def cache_kernel(y_ref, wk_ref, wv_ref, bv_ref, k_ref, v_ref, bias_ref):
    @pl.when(pl.program_id(0) == 0)
    def _():
        layers, width = bv_ref.shape
        columns = f32(bv_ref).T
        for layer in range(layers):
            bias_ref[layer * width:(layer + 1) * width, :] = columns[:, layer:layer + 1]

    cores, chips = y_ref.shape[1:3]
    rows = jnp.concatenate([y_ref[0, core, chip] for chip in range(chips) for core in range(cores)], axis=0)
    shape = k_ref.shape
    keys = lax.dot_general(wk_ref[...], rows, NT, preferred_element_type=jnp.float32)
    k_ref[...] = keys.astype(jnp.bfloat16).reshape(shape)
    values = lax.dot_general(wv_ref[...], rows, NT, preferred_element_type=jnp.float32) + bias_ref[...]
    v_ref[...] = values.astype(jnp.bfloat16).reshape(shape)


def whole(*shape):
    return pl.BlockSpec(shape, lambda i: (0,) * len(shape))


def solution(mesh):
    def device_fn(x_rows, ln1_gain, ln1_bias, w_query, b_query, w_key, w_value, b_value, w_out, b_out, ln2_gain, ln2_bias, w_up, b_up, w_down, b_down, lnp_gain, lnp_bias, cross_wk, cross_wv, cross_bv):
        batch, frames_dev, d_model = x_rows.shape
        layers, _, width = cross_wk.shape
        devices = lax.axis_size('sp')
        chips = devices // CORES
        frames_all = frames_dev * devices
        wide = w_up.shape[1]
        bf16 = jnp.bfloat16
        hbm = pl.BlockSpec(memory_space=pl.ANY)
        vmem = pl.BlockSpec(memory_space=pltpu.VMEM)
        per_clip = pltpu.SemaphoreType.DMA((5, batch))
        y_all = pl.pallas_call(
            encoder_kernel,
            in_specs=[hbm] * 7 + [vmem] * 11,
            out_specs=hbm,
            out_shape=jax.ShapeDtypeStruct((batch, CORES, chips, frames_dev, d_model), bf16),
            scratch_shapes=[
                pltpu.VMEM((batch, CORES, chips, frames_dev, d_model), bf16),
                pltpu.VMEM((batch, frames_dev, d_model), bf16),
                pltpu.VMEM((batch, frames_dev, d_model), bf16),
                pltpu.VMEM((d_model, d_model), bf16), pltpu.VMEM((d_model, d_model), bf16), pltpu.VMEM((d_model, d_model), bf16),
                pltpu.VMEM((d_model, d_model), bf16), pltpu.VMEM((d_model, d_model), bf16),
                pltpu.VMEM((d_model, wide), bf16), pltpu.VMEM((wide, d_model), bf16),
                pltpu.VMEM((d_model, frames_all), bf16), pltpu.VMEM((frames_all, d_model), bf16),
                pltpu.VMEM((frames_dev, d_model), bf16),
                pltpu.SemaphoreType.DMA((8,)), pltpu.SemaphoreType.DMA((batch,)),
                per_clip, per_clip, per_clip, per_clip,
            ],
            compiler_params=pltpu.CompilerParams(collective_id=0, has_side_effects=True, vmem_limit_bytes=VMEM_BYTES),
            name="encoder",
        )(x_rows, w_query, w_key, w_value, w_out, w_up, w_down, ln1_gain, ln1_bias, b_query, b_value, b_out,
          ln2_gain, ln2_bias, b_up, b_down, lnp_gain, lnp_bias)

        ckt = jnp.swapaxes(cross_wk, 1, 2).reshape(layers * width, d_model)
        cvt = jnp.swapaxes(cross_wv, 1, 2).reshape(layers * width, d_model)
        shape = jax.ShapeDtypeStruct((layers, batch, width, frames_all), bf16)
        wspec = whole(layers * width, d_model)
        blk = pl.BlockSpec((layers, 1, width, frames_all), lambda i: (0, i, 0, 0))
        held = pl.pallas_call(
            cache_kernel, grid=(batch,),
            in_specs=[pl.BlockSpec((1, CORES, chips, frames_dev, d_model), lambda i: (i, 0, 0, 0, 0)), wspec, wspec, whole(layers, width)],
            out_specs=[blk, blk], out_shape=[shape, shape],
            scratch_shapes=[pltpu.VMEM((layers * width, 1), jnp.float32)],
            compiler_params=pltpu.CompilerParams(dimension_semantics=("arbitrary",), vmem_limit_bytes=VMEM_BYTES),
            name="caches",
        )(y_all, ckt, cvt, cross_bv)
        heads = width // HEAD_DIM
        return tuple(jnp.moveaxis(buf.reshape(layers, batch, heads, HEAD_DIM, frames_all), 4, 2) for buf in held)

    in_specs = (P('dp', 'sp', None),) + (P(),) * 17 + (P(None, None, 'sp'), P(None, None, 'sp'), P(None, 'sp'))
    out_specs = (P(None, 'dp', None, 'sp', None), P(None, 'dp', None, 'sp', None))
    return jax.shard_map(device_fn, mesh=mesh, in_specs=in_specs, out_specs=out_specs, check_vma=False)
```

time: 683 us -> 255 us (0.37)
  matrix products: 305 us -> 0 us
  Pallas kernels: 0 us -> 253 us
  waiting for transfers between devices: 241 us -> 0 us
  local copies, waits for them, and re-layouts: 105 us -> 0 us
  other arithmetic: 16.4 us -> 0 us
  between operations: 14.3 us -> 0.65 us
    pallas_call x0 -> x2, Pallas kernels: none -> 253 us  [the longest x1 221 us: device_fn(): pl.pallas_call(encoder_kernel, in_specs=[hbm] * 7 + [vmem] * 11, out_spec...]
    all_gather x3 -> x0, waiting for transfers between devices: 241 us -> none  [the longest x1 119 us: device_fn(): y_all = lax.all_gather(y_local, 'sp', axis=1, tiled=True)]
    dot_general x9 -> x0, matrix products: 237 us -> none  [the longest x1 73 us: device_fn(): jnp.einsum('bfe,ed->bfd', hidden, w_down, preferred_element_type=jnp.floa...]
    sub x1 -> x0, matrix products: 67.6 us -> none  [device_fn(): attn_probs = jax.nn.softmax(scores, axis=-1).astype(jnp.bfloat16)]
    all_gather x2 -> x0, local copies, waits for them, and re-layouts: 65.3 us -> none  [the longest x1 32.6 us: device_fn(): key_all = lax.all_gather(key_rows, 'sp', axis=1, tiled=True)]
    unnamed x50 -> x0, local copies, waits for them, and re-layouts: 34.1 us -> none
    convert_element_type x13 -> x0, other arithmetic: 8.38 us -> none  [the longest x1 2.28 us: device_fn(): y_local = layer_norm(residual, lnp_gain, lnp_bias).astype(jnp.bfloat16)]
    reduce_sum x4 -> x0, other arithmetic: 8.03 us -> none  [the longest x3 5.36 us: layer_norm(): variance = jnp.mean(centered * centered, axis=-1, keepdims=True)]
  transfers between devices with their start and end apart: 3 -> 0, of which waited for: 3 -> 0; matrix products, arithmetic and copies ran while one was open for 18% -> 0% of each run, Pallas kernels for 0% -> 0%
where the time goes in v1:
time: 255 us; the launch traced here: 254 us
  Pallas kernels  253 us (99%)
    pallas_call x1, Pallas kernels, device_fn(): pl.pallas_call(encoder_kernel, in_specs=[hbm] * 7 + [vmem] * 11, out_spec...  221 us
    pallas_call x1, Pallas kernels, device_fn(): pl.pallas_call(cache_kernel, grid=(batch,), in_specs=[pl.BlockSpec((1, CO...  32.8 us

profile of v1, /device:TPU:81, one launch (start us, length us, event | category | flops | bytes accessed | tf_op | source)
XLA Modules:
  0.0 254.1 jit_solution(12086440585322864602)
XLA Ops:
  0.6 220.7 %encoder.1.y_ref = bf16[16,2,4,192,512]{4,3,2,1,0:T(8,128)(2,1)} custom-call(bf16[16,192,512]{2,1,0:T(8,128)(2,1)} %x_hbm.1, bf16[512,512]{1,0:T(8,128)(2,1)} %wq_hbm.1, bf16[512,512]{1,0:T(8,128)(2,1)} %wk_hbm.1, bf16[512,512]{1,0:T(8,128)(2,1)} %wv_hbm.1, bf16[512,512]{1,0:T(8,128)(2,1)} %wo_hbm.1, bf16[512,2048]{1,0:T(8,128)(2,1)} %wu_hbm.1, ...), custom_call_target="tpu_custom_call" | custom-call | tf_op jit(solution)/shard_map/encoder/pallas_call | solution.py:260
  221.3 32.8 %caches.1 = (bf16[6,16,64,1536]{3,2,1,0:T(8,128)(2,1)}, bf16[6,16,64,1536]{3,2,1,0:T(8,128)(2,1)}) custom-call(bf16[16,2,4,192,512]{4,3,2,1,0:T(8,128)(2,1)} %encoder.1.y_ref, bf16[384,512]{1,0:T(8,128)(2,1)} %bitcast.16, bf16[384,512]{1,0:T(8,128)(2,1)} %bitcast.17, bf16[6,64]{1,0:T(8,128)(2,1)} %bv_ref.3), custom_call_target="tpu_custom_call" | custom-call | tf_op jit(solution)/shard_map/caches/pallas_call | solution.py:287

commit v2 on v0

v2 whole, which is shorter than its diff:
```python
import functools
import jax
import jax.numpy as jnp
from jax import lax
from jax.experimental import pallas as pl
from jax.experimental.pallas import tpu as pltpu
from jax.sharding import PartitionSpec as P

HEAD_DIM = 64
LN_EPS = 1e-5
SQRT_HALF = 0.5 ** 0.5
PAIR = 2 * HEAD_DIM
VMEM_BYTES = 63 * 1024 * 1024
CORES = 2
KINDS = 13
RELAY_LAG = 2
PUSH_LAG = 4
MESH_ID = pl.DeviceIdType.MESH
NT = (((1,), (1,)), ((), ()))


def norm_rows(rows, gain, bias):
    mean_val = jnp.mean(rows, axis=-1, keepdims=True)
    centered = rows - mean_val
    variance = jnp.mean(centered * centered, axis=-1, keepdims=True)
    return centered * lax.rsqrt(variance + LN_EPS) * gain + bias


def f32(ref):
    return ref[...].astype(jnp.float32)


def vec(ref):
    return f32(ref).reshape(1, ref.shape[0])


def encoder_kernel(x_hbm, wq_hbm, wk_hbm, wv_hbm, wo_hbm, wu_hbm, wd_hbm,
                   gain1_ref, bias1_ref, bq_ref, bv_ref, bo_ref, gain2_ref, bias2_ref, bu_ref, bd_ref, gainp_ref, biasp_ref,
                   y_all, x_buf, relay_buf, y_buf, wq_ref, wk_ref, wkt_ref, wv_ref, wo_ref, wu_ref, wd_ref, a_ref, q_ref, kt_ref, v_ref, att_ref,
                   load_sem, keep_sem, x_send, x_recv, y_send, y_recv):
    chips, _, per, blocks, frames, d_model = y_all.shape
    half = frames // 2
    items = per * blocks
    me = lax.axis_index('sp')
    core, chip = lax.rem(me, CORES), lax.div(me, CORES)
    other = 1 - core
    rchip, lchip, far = lax.rem(chip + 1, chips), lax.rem(chip + chips - 1, chips), lax.rem(chip + 2, chips)
    right, left, partner = {'sp': rchip * CORES + core}, {'sp': lchip * CORES + core}, {'sp': chip * CORES + other}

    mine = [pltpu.make_async_copy(x_hbm.at[me * per + c], x_buf.at[c, me], load_sem.at[c]) for c in range(per)]
    pairs = ((wq_hbm, wq_ref), (wk_hbm, wk_ref), (wv_hbm, wv_ref), (wo_hbm, wo_ref), (wu_hbm, wu_ref), (wd_hbm, wd_ref))
    loads = [pltpu.make_async_copy(src, dst, load_sem.at[per + i]) for i, (src, dst) in enumerate(pairs)]

    around = [where * CORES + k for where in (rchip, lchip) for k in range(CORES)] + [chip * CORES + other]
    barrier = pltpu.get_barrier_semaphore()
    for peer in around:
        pl.semaphore_signal(barrier, inc=1, device_id={'sp': peer}, device_id_type=MESH_ID)
    pl.semaphore_wait(barrier, len(around))

    def remote(src, dst, send, recv, peer):
        return pltpu.make_async_remote_copy(src_ref=src, dst_ref=dst, send_sem=send, recv_sem=recv, device_id=peer, device_id_type=MESH_ID)

    rows_lo, rows_hi = pl.ds(0, half), pl.ds(half, half)

    def scatter(c):
        def link(kind, src, dst, mark, peer):
            return remote(src, dst, x_send.at[c, kind], x_recv.at[c, mark], {'sp': peer})

        copies = []
        for k in range(CORES):
            away = x_hbm.at[(far * CORES + k) * per + c]
            copies.append(link(5 + k, away.at[rows_lo], relay_buf.at[0, c, k], 5 + k, rchip * CORES + core))
            copies.append(link(7 + k, away.at[rows_hi], relay_buf.at[1, c, k], 7 + k, lchip * CORES + core))
        for k in range(CORES):
            copies.append(link(1 + k, x_hbm.at[(rchip * CORES + k) * per + c], x_buf.at[c, me], 1 + core, rchip * CORES + k))
            copies.append(link(3 + k, x_hbm.at[(lchip * CORES + k) * per + c], x_buf.at[c, me], 3 + core, lchip * CORES + k))
        copies.append(link(0, x_hbm.at[(chip * CORES + other) * per + c], x_buf.at[c, me], 0, chip * CORES + other))
        return copies

    def onward(c):
        pairs = []
        for k in range(CORES):
            to_right = x_buf.at[c, lchip * CORES + core, rows_lo]
            to_left = x_buf.at[c, rchip * CORES + core, rows_hi]
            came_left, came_right = relay_buf.at[0, c, k], relay_buf.at[1, c, k]
            pairs.append((lambda ref=came_left, mark=5 + k: remote(ref, ref, x_send.at[c, mark], x_recv.at[c, mark], right).wait_recv(),
                          remote(came_left, to_right, x_send.at[c, 9 + k], x_recv.at[c, 9 + core], {'sp': rchip * CORES + k})))
            pairs.append((lambda ref=came_right, mark=7 + k: remote(ref, ref, x_send.at[c, mark], x_recv.at[c, mark], right).wait_recv(),
                          remote(came_right, to_left, x_send.at[c, 11 + k], x_recv.at[c, 11 + core], {'sp': lchip * CORES + k})))
        return pairs

    def send_clip(c):
        for copy in scatter(c):
            copy.start()

    def relay_clip(c):
        for came, goes in onward(c):
            came()
            goes.start()

    def arrivals(c):
        def landed(mark, ref):
            return remote(ref, ref, x_send.at[c, mark], x_recv.at[c, mark], right)

        near = [(0, chip * CORES + other)]
        near += [(1 + k, lchip * CORES + k) for k in range(CORES)] + [(3 + k, rchip * CORES + k) for k in range(CORES)]
        groups = [(block, [landed(mark, x_buf.at[c, block])]) for mark, block in near]
        for k in range(CORES):
            block = far * CORES + k
            groups.append((block, [landed(9 + k, x_buf.at[c, block, rows_lo]), landed(11 + k, x_buf.at[c, block, rows_hi])]))
        return groups

    send_clip(0)
    for copy in mine:
        copy.start()
    for load in loads:
        load.start()

    def place(t, where):
        return y_all.at[where, core, lax.div(t, blocks), lax.rem(t, blocks)]

    def lower(t, where):
        return y_all.at[where, core, lax.div(t, blocks), lax.rem(t, blocks), pl.ds(0, half)]

    def upper(t, where):
        return y_all.at[where, core, lax.div(t, blocks), lax.rem(t, blocks), pl.ds(half, half)]

    def column(t, side):
        return y_all.at[pl.ds(0, chips), side, lax.div(t, blocks), lax.rem(t, blocks)]

    def out_right(t):
        return remote(y_buf.at[t], place(t, chip), y_send.at[0, t], y_recv.at[0, t], right)

    def out_left(t):
        return remote(y_buf.at[t], place(t, chip), y_send.at[1, t], y_recv.at[1, t], left)

    def fwd_right(t):
        return remote(lower(t, lchip), lower(t, lchip), y_send.at[2, t], y_recv.at[2, t], right)

    def fwd_left(t):
        return remote(upper(t, rchip), upper(t, rchip), y_send.at[3, t], y_recv.at[3, t], left)

    def across(t):
        return remote(column(t, core), column(t, core), y_send.at[4, t], y_recv.at[4, t], partner)

    def keep(t):
        return pltpu.make_async_copy(y_buf.at[t], place(t, chip), keep_sem.at[t])

    def first(t):
        keep(t).start()
        out_right(t).start()
        out_left(t).start()

    def relay(t):
        remote(place(t, lchip), place(t, lchip), y_send.at[0, t], y_recv.at[0, t], right).wait_recv()
        fwd_right(t).start()
        remote(place(t, rchip), place(t, rchip), y_send.at[1, t], y_recv.at[1, t], left).wait_recv()
        fwd_left(t).start()

    def push(t):
        keep(t).wait()
        remote(lower(t, far), lower(t, far), y_send.at[2, t], y_recv.at[2, t], right).wait_recv()
        remote(upper(t, far), upper(t, far), y_send.at[3, t], y_recv.at[3, t], left).wait_recv()
        across(t).start()

    qk_scale = HEAD_DIM ** -0.25
    low = lax.broadcasted_iota(jnp.int32, (half, PAIR), 1) < HEAD_DIM
    gain1, bias1 = vec(gain1_ref), vec(bias1_ref)

    def norm(c, block):
        a_ref[block] = norm_rows(x_buf[c, block].astype(jnp.float32), gain1, bias1).astype(jnp.bfloat16)

    def project():
        rows = a_ref[...].reshape(blocks * frames, d_model)
        queries = ((jnp.dot(rows, wq_ref[...], preferred_element_type=jnp.float32) + vec(bq_ref)) * qk_scale).astype(jnp.bfloat16)
        q_ref[...] = queries.reshape(blocks, frames, d_model)
        kt_ref[...] = (lax.dot_general(wkt_ref[...], rows, NT, preferred_element_type=jnp.float32) * qk_scale).astype(jnp.bfloat16)
        v_ref[...] = (jnp.dot(rows, wv_ref[...], preferred_element_type=jnp.float32) + vec(bv_ref)).astype(jnp.bfloat16)

    def attention(block):
        tasks = [(pair, piece, side) for pair in range(d_model // PAIR) for piece in range(2) for side in range(2)]
        held = {}

        def score(task):
            pair, piece, side = task
            cols = slice(pair * PAIR, (pair + 1) * PAIR)
            q_pair = q_ref[block, piece * half:(piece + 1) * half, cols]
            q_head = jnp.where(low if side == 0 else jnp.logical_not(low), q_pair, jnp.zeros_like(q_pair))
            return jnp.dot(q_head, kt_ref[cols, :], preferred_element_type=jnp.float32)

        def soften(scores):
            top = jnp.max(scores, axis=-1, keepdims=True)
            weights = jnp.exp(scores - top)
            return weights.astype(jnp.bfloat16), jnp.sum(weights, axis=-1, keepdims=True)

        def mix(task, weights, total):
            pair, piece, side = task
            cols = slice(pair * PAIR, (pair + 1) * PAIR)
            out = jnp.dot(weights, v_ref[:, cols], preferred_element_type=jnp.float32) / total
            if side == 0:
                held[0] = out
            else:
                att_ref[piece * half:(piece + 1) * half, cols] = jnp.where(low, held[0], out).astype(jnp.bfloat16)

        scores, waiting = score(tasks[0]), None
        for i, task in enumerate(tasks):
            following = score(tasks[i + 1]) if i + 1 < len(tasks) else None
            weights, total = soften(scores)
            if waiting is not None:
                mix(*waiting)
            waiting, scores = (task, weights, total), following
        mix(*waiting)

    def feed_forward(c, block, t):
        residual = x_buf[c, block].astype(jnp.float32)
        residual = residual + jnp.dot(att_ref[...], wo_ref[...], preferred_element_type=jnp.float32) + vec(bo_ref)
        normed = norm_rows(residual, vec(gain2_ref), vec(bias2_ref)).astype(jnp.bfloat16)
        hidden = []
        for start in range(0, wu_ref.shape[1], d_model):
            cols = slice(start, start + d_model)
            up = jnp.dot(normed, wu_ref[:, cols], preferred_element_type=jnp.float32) + bu_ref[cols].astype(jnp.float32).reshape(1, d_model)
            halved = 0.5 * up
            hidden.append((halved + halved * lax.erf(up * SQRT_HALF)).astype(jnp.bfloat16))
        acc = residual + jnp.dot(jnp.concatenate(hidden, axis=1), wd_ref[...], preferred_element_type=jnp.float32) + vec(bd_ref)
        y_buf[t] = norm_rows(acc, vec(gainp_ref), vec(biasp_ref)).astype(jnp.bfloat16)

    relay_clip(0)
    if per > 1:
        send_clip(1)
    for load in loads:
        load.wait()
    wkt_ref[...] = wk_ref[...].T

    @pl.loop(0, per)
    def _(c):
        pltpu.make_async_copy(x_hbm.at[me * per + c], x_buf.at[c, me], load_sem.at[c]).wait()
        norm(c, me)
        for block, copies in arrivals(c):
            for copy in copies:
                copy.wait_recv()
            norm(c, block)
        project()

        @pl.when(c + 1 < per)
        def _():
            relay_clip(c + 1)

        @pl.when(c + 2 < per)
        def _():
            send_clip(c + 2)

        @pl.loop(0, blocks)
        def _(block):
            t = c * blocks + block
            attention(block)

            @pl.when(t >= RELAY_LAG)
            def _():
                relay(t - RELAY_LAG)

            feed_forward(c, block, t)
            first(t)

            @pl.when(t >= PUSH_LAG)
            def _():
                push(t - PUSH_LAG)

    for back in range(PUSH_LAG, 0, -1):
        if back <= RELAY_LAG:
            relay(items - back)
    for back in range(PUSH_LAG, 0, -1):
        push(items - back)

    @pl.loop(0, items)
    def _(t):
        remote(column(t, other), column(t, other), y_send.at[4, t], y_recv.at[4, t], partner).wait_recv()
        for copy in (out_right(t), out_left(t), fwd_right(t), fwd_left(t), across(t)):
            copy.wait_send()

    @pl.loop(0, per)
    def _(c):
        for copy in scatter(c):
            copy.wait_send()
        for _, goes in onward(c):
            goes.wait_send()


def cache_kernel(y_ref, wk_ref, wv_ref, bv_ref, k_ref, v_ref, bias_ref):
    @pl.when(pl.program_id(0) == 0)
    def _():
        layers, width = bv_ref.shape
        columns = f32(bv_ref).T
        for layer in range(layers):
            bias_ref[layer * width:(layer + 1) * width, :] = columns[:, layer:layer + 1]

    rows = y_ref[0]
    shape = k_ref.shape
    keys = lax.dot_general(wk_ref[...], rows, NT, preferred_element_type=jnp.float32)
    k_ref[...] = keys.astype(jnp.bfloat16).reshape(shape)
    values = lax.dot_general(wv_ref[...], rows, NT, preferred_element_type=jnp.float32) + bias_ref[...]
    v_ref[...] = values.astype(jnp.bfloat16).reshape(shape)


def whole(*shape):
    return pl.BlockSpec(shape, lambda i: (0,) * len(shape))


def solution(mesh):
    def device_fn(x_rows, ln1_gain, ln1_bias, w_query, b_query, w_key, w_value, b_value, w_out, b_out, ln2_gain, ln2_bias, w_up, b_up, w_down, b_down, lnp_gain, lnp_bias, cross_wk, cross_wv, cross_bv):
        batch, frames_dev, d_model = x_rows.shape
        layers, _, width = cross_wk.shape
        devices = lax.axis_size('sp')
        chips = devices // CORES
        frames_all = frames_dev * devices
        wide = w_up.shape[1]
        bf16 = jnp.bfloat16
        hbm = pl.BlockSpec(memory_space=pl.ANY)
        vmem = pl.BlockSpec(memory_space=pltpu.VMEM)
        per = batch // devices
        clip_rows = pltpu.VMEM((devices, frames_dev, d_model), bf16)
        square = pltpu.VMEM((d_model, d_model), bf16)
        y_all = pl.pallas_call(
            encoder_kernel,
            in_specs=[hbm] * 7 + [vmem] * 11,
            out_specs=hbm,
            out_shape=jax.ShapeDtypeStruct((chips, CORES, per, devices, frames_dev, d_model), bf16),
            scratch_shapes=[
                pltpu.VMEM((per, devices, frames_dev, d_model), bf16),
                pltpu.VMEM((2, per, CORES, frames_dev // 2, d_model), bf16),
                pltpu.VMEM((batch, frames_dev, d_model), bf16),
                square, square, square, square, square,
                pltpu.VMEM((d_model, wide), bf16), pltpu.VMEM((wide, d_model), bf16),
                clip_rows, clip_rows,
                pltpu.VMEM((d_model, frames_all), bf16), pltpu.VMEM((frames_all, d_model), bf16),
                pltpu.VMEM((frames_dev, d_model), bf16),
                pltpu.SemaphoreType.DMA((per + 6,)), pltpu.SemaphoreType.DMA((batch,)),
                pltpu.SemaphoreType.DMA((per, KINDS)), pltpu.SemaphoreType.DMA((per, KINDS)),
                pltpu.SemaphoreType.DMA((5, batch)), pltpu.SemaphoreType.DMA((5, batch)),
            ],
            compiler_params=pltpu.CompilerParams(collective_id=0, has_side_effects=True, vmem_limit_bytes=VMEM_BYTES),
            name="encoder",
        )(x_rows, w_query, w_key, w_value, w_out, w_up, w_down, ln1_gain, ln1_bias, b_query, b_value, b_out,
          ln2_gain, ln2_bias, b_up, b_down, lnp_gain, lnp_bias)
        y_all = y_all.reshape(batch, frames_all, d_model)

        ckt = jnp.swapaxes(cross_wk, 1, 2).reshape(layers * width, d_model)
        cvt = jnp.swapaxes(cross_wv, 1, 2).reshape(layers * width, d_model)
        shape = jax.ShapeDtypeStruct((layers, batch, width, frames_all), bf16)
        wspec = whole(layers * width, d_model)
        blk = pl.BlockSpec((layers, 1, width, frames_all), lambda i: (0, i, 0, 0))
        held = pl.pallas_call(
            cache_kernel, grid=(batch,),
            in_specs=[pl.BlockSpec((1, frames_all, d_model), lambda i: (i, 0, 0)), wspec, wspec, whole(layers, width)],
            out_specs=[blk, blk], out_shape=[shape, shape],
            scratch_shapes=[pltpu.VMEM((layers * width, 1), jnp.float32)],
            compiler_params=pltpu.CompilerParams(dimension_semantics=("arbitrary",), vmem_limit_bytes=VMEM_BYTES),
            name="caches",
        )(y_all, ckt, cvt, cross_bv)
        heads = width // HEAD_DIM
        return tuple(jnp.moveaxis(buf.reshape(layers, batch, heads, HEAD_DIM, frames_all), 4, 2) for buf in held)

    in_specs = (P('dp', 'sp', None),) + (P(),) * 17 + (P(None, None, 'sp'), P(None, None, 'sp'), P(None, 'sp'))
    out_specs = (P(None, 'dp', None, 'sp', None), P(None, 'dp', None, 'sp', None))
    return jax.shard_map(device_fn, mesh=mesh, in_specs=in_specs, out_specs=out_specs, check_vma=False)
```

time: 683 us -> 180 us (0.26)
  matrix products: 305 us -> 0 us
  waiting for transfers between devices: 241 us -> 0 us
  Pallas kernels: 0 us -> 179 us
  local copies, waits for them, and re-layouts: 105 us -> 0 us
  other arithmetic: 16.4 us -> 0 us
  between operations: 14.3 us -> 0.65 us
    all_gather x3 -> x0, waiting for transfers between devices: 241 us -> none  [the longest x1 119 us: device_fn(): y_all = lax.all_gather(y_local, 'sp', axis=1, tiled=True)]
    dot_general x9 -> x0, matrix products: 237 us -> none  [the longest x1 73 us: device_fn(): jnp.einsum('bfe,ed->bfd', hidden, w_down, preferred_element_type=jnp.floa...]
    pallas_call x0 -> x2, Pallas kernels: none -> 179 us  [the longest x1 146 us: device_fn(): pl.pallas_call(encoder_kernel, in_specs=[hbm] * 7 + [vmem] * 11, out_spec...]
    sub x1 -> x0, matrix products: 67.6 us -> none  [device_fn(): attn_probs = jax.nn.softmax(scores, axis=-1).astype(jnp.bfloat16)]
    all_gather x2 -> x0, local copies, waits for them, and re-layouts: 65.3 us -> none  [the longest x1 32.6 us: device_fn(): key_all = lax.all_gather(key_rows, 'sp', axis=1, tiled=True)]
    unnamed x50 -> x0, local copies, waits for them, and re-layouts: 34.1 us -> none
    convert_element_type x13 -> x0, other arithmetic: 8.38 us -> none  [the longest x1 2.28 us: device_fn(): y_local = layer_norm(residual, lnp_gain, lnp_bias).astype(jnp.bfloat16)]
    reduce_sum x4 -> x0, other arithmetic: 8.03 us -> none  [the longest x3 5.36 us: layer_norm(): variance = jnp.mean(centered * centered, axis=-1, keepdims=True)]
  transfers between devices with their start and end apart: 3 -> 0, of which waited for: 3 -> 0; matrix products, arithmetic and copies ran while one was open for 18% -> 0% of each run, Pallas kernels for 0% -> 0%
where the time goes in v2:
time: 180 us
  Pallas kernels  179 us (99%)
    pallas_call x1, Pallas kernels, device_fn(): pl.pallas_call(encoder_kernel, in_specs=[hbm] * 7 + [vmem] * 11, out_spec...  146 us
    pallas_call x1, Pallas kernels, device_fn(): pl.pallas_call(cache_kernel, grid=(batch,), in_specs=[pl.BlockSpec((1, fr...  32.8 us

profile of v2, /device:TPU:81, one launch (start us, length us, event | category | flops | bytes accessed | tf_op | source)
XLA Modules:
  0.0 179.6 jit_solution(18224395085335406404)
XLA Ops:
  0.6 146.2 %encoder.1 = bf16[4,2,2,8,192,512]{5,4,3,2,1,0:T(8,128)(2,1)} custom-call(bf16[16,192,512]{2,1,0:T(8,128)(2,1)} %x_hbm.1, bf16[512,512]{1,0:T(8,128)(2,1)} %wq_hbm.1, bf16[512,512]{1,0:T(8,128)(2,1)} %wk_hbm.1, bf16[512,512]{1,0:T(8,128)(2,1)} %wv_hbm.1, bf16[512,512]{1,0:T(8,128)(2,1)} %wo_hbm.1, bf16[512,2048]{1,0:T(8,128)(2,1)} %wu_hbm.1, ...), custom_call_target="tpu_custom_call" | custom-call | tf_op jit(solution)/shard_map/encoder/pallas_call | solution.py:322
  146.9 32.8 %caches.1 = (bf16[6,16,64,1536]{3,2,1,0:T(8,128)(2,1)}, bf16[6,16,64,1536]{3,2,1,0:T(8,128)(2,1)}) custom-call(bf16[16,1536,512]{2,1,0:T(8,128)(2,1)} %bitcast.17, bf16[384,512]{1,0:T(8,128)(2,1)} %bitcast.18, bf16[384,512]{1,0:T(8,128)(2,1)} %bitcast.19, bf16[6,64]{1,0:T(8,128)(2,1)} %bv_ref.3), custom_call_target="tpu_custom_call" | custom-call | tf_op jit(solution)/shard_map/caches/pallas_call | solution.py:351

commit v3 on v2

--- a/solution.py
+++ b/solution.py
@@ -285,24 +285,50 @@
             goes.wait_send()
 
 
-def cache_kernel(y_ref, wk_ref, wv_ref, bv_ref, k_ref, v_ref, bias_ref):
-    @pl.when(pl.program_id(0) == 0)
-    def _():
-        layers, width = bv_ref.shape
-        columns = f32(bv_ref).T
-        for layer in range(layers):
-            bias_ref[layer * width:(layer + 1) * width, :] = columns[:, layer:layer + 1]
-
-    rows = y_ref[0]
-    shape = k_ref.shape
-    keys = lax.dot_general(wk_ref[...], rows, NT, preferred_element_type=jnp.float32)
-    k_ref[...] = keys.astype(jnp.bfloat16).reshape(shape)
-    values = lax.dot_general(wv_ref[...], rows, NT, preferred_element_type=jnp.float32) + bias_ref[...]
-    v_ref[...] = values.astype(jnp.bfloat16).reshape(shape)
-
-
-def whole(*shape):
-    return pl.BlockSpec(shape, lambda i: (0,) * len(shape))
+def cache_kernel(y_hbm, wk_ref, wv_ref, bv_ref, k_hbm, v_hbm, bias_ref, y_buf, k_buf, v_buf, in_sem, k_sem, v_sem):
+    clips, depth = y_hbm.shape[0], y_buf.shape[0]
+    layers, width = bv_ref.shape
+    held = k_buf.shape[1:]
+
+    def load(clip):
+        slot = lax.rem(clip, depth)
+        return pltpu.make_async_copy(y_hbm.at[clip], y_buf.at[slot], in_sem.at[slot])
+
+    def store(buf, out, sem, clip):
+        slot = lax.rem(clip, 2)
+        return pltpu.make_async_copy(buf.at[slot], out.at[pl.ds(0, layers), clip], sem.at[slot])
+
+    for clip in range(depth - 1):
+        load(clip).start()
+    columns = f32(bv_ref).T
+    for layer in range(layers):
+        bias_ref[layer * width:(layer + 1) * width, :] = columns[:, layer:layer + 1]
+
+    @pl.loop(0, clips)
+    def _(clip):
+        load(clip).wait()
+
+        @pl.when(clip + depth - 1 < clips)
+        def _():
+            load(clip + depth - 1).start()
+
+        @pl.when(clip >= 2)
+        def _():
+            store(k_buf, k_hbm, k_sem, clip - 2).wait()
+            store(v_buf, v_hbm, v_sem, clip - 2).wait()
+
+        slot = lax.rem(clip, 2)
+        rows = y_buf[lax.rem(clip, depth)]
+        keys = lax.dot_general(wk_ref[...], rows, NT, preferred_element_type=jnp.float32)
+        k_buf[slot] = keys.astype(jnp.bfloat16).reshape(held)
+        store(k_buf, k_hbm, k_sem, clip).start()
+        values = lax.dot_general(wv_ref[...], rows, NT, preferred_element_type=jnp.float32) + bias_ref[...]
+        v_buf[slot] = values.astype(jnp.bfloat16).reshape(held)
+        store(v_buf, v_hbm, v_sem, clip).start()
+
+    for clip in range(clips - 2, clips):
+        store(k_buf, k_hbm, k_sem, clip).wait()
+        store(v_buf, v_hbm, v_sem, clip).wait()
 
 
 def solution(mesh):
@@ -346,14 +372,16 @@
         ckt = jnp.swapaxes(cross_wk, 1, 2).reshape(layers * width, d_model)
         cvt = jnp.swapaxes(cross_wv, 1, 2).reshape(layers * width, d_model)
         shape = jax.ShapeDtypeStruct((layers, batch, width, frames_all), bf16)
-        wspec = whole(layers * width, d_model)
-        blk = pl.BlockSpec((layers, 1, width, frames_all), lambda i: (0, i, 0, 0))
+        out_buf = pltpu.VMEM((2, layers, width, frames_all), bf16)
         held = pl.pallas_call(
-            cache_kernel, grid=(batch,),
-            in_specs=[pl.BlockSpec((1, frames_all, d_model), lambda i: (i, 0, 0)), wspec, wspec, whole(layers, width)],
-            out_specs=[blk, blk], out_shape=[shape, shape],
-            scratch_shapes=[pltpu.VMEM((layers * width, 1), jnp.float32)],
-            compiler_params=pltpu.CompilerParams(dimension_semantics=("arbitrary",), vmem_limit_bytes=VMEM_BYTES),
+            cache_kernel,
+            in_specs=[hbm, vmem, vmem, vmem],
+            out_specs=[hbm, hbm], out_shape=[shape, shape],
+            scratch_shapes=[
+                pltpu.VMEM((layers * width, 1), jnp.float32), pltpu.VMEM((4, frames_all, d_model), bf16), out_buf, out_buf,
+                pltpu.SemaphoreType.DMA((4,)), pltpu.SemaphoreType.DMA((2,)), pltpu.SemaphoreType.DMA((2,)),
+            ],
+            compiler_params=pltpu.CompilerParams(vmem_limit_bytes=VMEM_BYTES),
             name="caches",
         )(y_all, ckt, cvt, cross_bv)
         heads = width // HEAD_DIM

time: 180 us -> 174 us (0.967)
  Pallas kernels: 179 us -> 173 us
    pallas_call x1, Pallas kernels: 32.8 us -> 26.6 us  [device_fn(): pl.pallas_call(cache_kernel, in_specs=[hbm, vmem, vmem, vmem], out_specs=...]
where the time goes in v3:
time: 174 us
  Pallas kernels  173 us (99%)
    pallas_call x1, Pallas kernels, device_fn(): pl.pallas_call(encoder_kernel, in_specs=[hbm] * 7 + [vmem] * 11, out_spec...  146 us
    pallas_call x1, Pallas kernels, device_fn(): pl.pallas_call(cache_kernel, in_specs=[hbm, vmem, vmem, vmem], out_specs=...  26.6 us

profile of v3, /device:TPU:81, one launch (start us, length us, event | category | flops | bytes accessed | tf_op | source)
XLA Modules:
  0.0 173.5 jit_solution(1298036544605482657)
XLA Ops:
  0.6 146.2 %encoder.1 = bf16[4,2,2,8,192,512]{5,4,3,2,1,0:T(8,128)(2,1)} custom-call(bf16[16,192,512]{2,1,0:T(8,128)(2,1)} %x_hbm.1, bf16[512,512]{1,0:T(8,128)(2,1)} %wq_hbm.1, bf16[512,512]{1,0:T(8,128)(2,1)} %wk_hbm.1, bf16[512,512]{1,0:T(8,128)(2,1)} %wv_hbm.1, bf16[512,512]{1,0:T(8,128)(2,1)} %wo_hbm.1, bf16[512,2048]{1,0:T(8,128)(2,1)} %wu_hbm.1, ...), custom_call_target="tpu_custom_call" | custom-call | tf_op jit(solution)/shard_map/encoder/pallas_call | solution.py:348
  146.9 26.6 %caches.1 = (bf16[6,16,64,1536]{3,2,1,0:T(8,128)(2,1)}, bf16[6,16,64,1536]{3,2,1,0:T(8,128)(2,1)}) custom-call(bf16[16,1536,512]{2,1,0:T(8,128)(2,1)} %bitcast.17, bf16[384,512]{1,0:T(8,128)(2,1)} %bitcast.18, bf16[384,512]{1,0:T(8,128)(2,1)} %bitcast.19, bf16[6,64]{1,0:T(8,128)(2,1)} %bv_ref.3), custom_call_target="tpu_custom_call" | custom-call | tf_op jit(solution)/shard_map/caches/pallas_call | solution.py:376
